TPU v7x, 32 devices: a whole 2x2x4 slice. The times are simulated.
32 devices in a mesh: rep: 2 (over x), dp: 16 (over y, z, core).
Axes of the slice: x: 2, y: 2, z: 4, core: 2. Of those that a mesh axis runs over, the one named last changes fastest.
Arguments:
- a: bfloat16 [32, 4, 8192, 896], P(('rep', 'dp')), parts along dimension 0
- g: bfloat16 [32, 4, 8192, 2560], P(('rep', 'dp')), parts along dimension 0
Outputs:
- output: bfloat16 [8, 896, 2560], P('rep'), parts along dimension 0
There are 2 independent parts. A program takes and returns all parts, laid end to end along the dimension named above; each array names one.
All inputs are finite; a program needn't handle non-finite values.
Results may differ from a plain program's by a relative error of at most 0.012.
Values are sent between devices in bfloat16 or wider.
A program may use at most 2 GiB of HBM per device.

v0:
```python
import jax
import jax.numpy as jnp


def solution(mesh):
    groups = mesh.shape["rep"]

    def step(a, g):
        a, g = (t.reshape(groups, -1, *t.shape[1:]) for t in (a, g))
        sums = jnp.einsum("rsntd,rsntf->rndf", a, g, preferred_element_type=jnp.float32)
        return sums.astype(jnp.bfloat16).reshape(-1, *sums.shape[2:])

    return step
```

profile of v0, /device:TPU:0, one launch (start us, length us, event | category | flops | bytes accessed | tf_op | source)
XLA Modules:
  0.0 925.0 jit_solution(7277524600718541724)
XLA Ops:
  0.0 166.8 %fusion.3 = f32[1,4,896,2560]{3,2,1,0:T(8,128)} fusion(bf16[1,4,8192,2560]{3,2,1,0:T(8,128)(2,1)} %param.1, bf16[1,4,8192,896]{3,2,1,0:T(8,128)(2,1)} %param), kind=kOutput, calls=%fused_computation.3 | convolution fusion | flops 150323855360 | bytes 263192576 | tf_op jit(solution)/rsntd,rsntf->rndf/dot_general | solution.py:10
  166.8 758.2 %all-reduce.2 = bf16[1,4,896,2560]{3,2,1,0:T(8,128)(2,1)} all-reduce(f32[1,4,896,2560]{3,2,1,0:T(8,128)} %fusion.3), channel_id=1, replica_groups=[2,16]<=[32], use_global_device_ids=true, to_apply=%add.clone | all-reduce | flops 9175040 | bytes 55050240 | tf_op jit(solution)/rsntd,rsntf->rndf/dot_general | solution.py:10
where the time goes:
time: 926 us; the launch traced here: 925 us
  blocking collectives  758 us (82%)
  matrix products  167 us (18%)
    dot_general x1, blocking collectives, step(): jnp.einsum('rsntd,rsntf->rndf', a, g, preferred_element_type=jnp.float32)  758 us
    dot_general x1, matrix products, step(): jnp.einsum('rsntd,rsntf->rndf', a, g, preferred_element_type=jnp.float32)  167 us

commit v1 on v0

v1 whole, which is shorter than its diff:
```python
import jax
import jax.numpy as jnp
from jax import lax
from jax.experimental import pallas as pl
from jax.experimental.pallas import tpu as pltpu
from jax.sharding import PartitionSpec as P

MESH = pl.DeviceIdType.MESH
F32, BF16 = jnp.float32, jnp.bfloat16

COLS = 256
DEPTH = 4096
GBUFS = 3
ASLABS = 8
SLOTS = 4
FSLOTS = 8
LAGS = dict(a1=3, a2t1=5, a2t2=6, a3t1=7, a3t2=8, a4t1=9, a4t2=10, a5t1=11, a5t2=12, a6=14, a7=16)
KINDS = ("core", "y", "q", "p", "w", "x", "t", "fe1", "fy", "f2m", "fe2", "fe3", "out", "loc")
KIND = {name: i for i, name in enumerate(KINDS)}


def kernel(
    a, g, o, abuf, gbuf, acc, sb0, rb0, sby, ry, sbq, rq, sbp, rp, sbw, rw, sbx, rx, sbt, rt, fin,
    keep_p, keep_q, keep_w, asem, gsem, ssem, rsem,
):
    mats, tokens, rows = a.shape[1:]
    ff = g.shape[3]
    nk, nj = tokens // DEPTH, ff // COLS
    blocks = mats * nj
    half, part = rows // 2, rows // 8
    slab = tokens // ASLABS
    per_dot = ASLABS // nk

    me = lax.axis_index("dp")
    c, z, y = me % 2, (me // 2) % 4, me // 8
    mid = (z == 1) | (z == 2)
    end = jnp.logical_not(mid)
    i = z // 2

    def at(y, z, c):
        return (y * 4 + z) * 2 + c

    sib, across = at(y, z, 1 - c), at(1 - y, z, c)
    inner, partner, outer = at(y, 1 + i, c), at(y, 3 - z, c), at(y, i * 3, c)

    def rc(kind, slot, src, dst, dev):
        return pltpu.make_async_remote_copy(
            src_ref=src, dst_ref=dst, send_sem=ssem.at[KIND[kind], slot], recv_sem=rsem.at[KIND[kind], slot],
            device_id={"dp": dev}, device_id_type=MESH,
        )

    def gcopy(s):
        b, k = s // nk, s % nk
        n, j = b // nj, b % nj
        return pltpu.make_async_copy(
            g.at[0, n, pl.ds(pl.multiple_of(k * DEPTH, DEPTH), DEPTH), pl.ds(pl.multiple_of(j * COLS, COLS), COLS)],
            gbuf.at[s % GBUFS], gsem.at[s % GBUFS],
        )

    def acopy(n, s):
        return pltpu.make_async_copy(
            a.at[0, n, pl.ds(pl.multiple_of(s * slab, slab), slab), :],
            abuf.at[n % 2, pl.ds(pl.multiple_of(s * slab, slab), slab), :], asem.at[n % 2, s],
        )

    def piece(first):
        return pl.ds(pl.multiple_of(first * part, part), part)

    def c_core(k):
        s = k % SLOTS
        return rc("core", s, sb0.at[s], rb0.at[s], sib)

    def c_y(k):
        s = k % SLOTS
        return rc("y", s, sby.at[s], ry.at[s], across)

    def c_q(k):
        s = k % SLOTS
        return rc("q", s, sbq.at[s], rq.at[s], inner)

    def c_p(k):
        s = k % SLOTS
        return rc("p", s, sbp.at[s], rp.at[s], inner)

    def c_w(k):
        s = k % SLOTS
        return rc("w", s, sbw.at[s], rw.at[s], partner)

    def c_x(k):
        s = k % SLOTS
        return rc("x", s, sbx.at[s], rx.at[s], partner)

    def c_t(k):
        s = k % SLOTS
        return rc("t", s, sbt.at[s], rt.at[s], across)

    def c_fin(kind, k, which, dev):
        s = k % FSLOTS
        return rc(kind, s, fin.at[s, piece(which), :], fin.at[s, piece(which), :], dev)

    def place(k):
        n, j = k // nj, k % nj
        return o.at[n, pl.ds(pl.multiple_of(c * half, half), half), pl.ds(pl.multiple_of(j * COLS, COLS), COLS)]

    def other_place(k):
        n, j = k // nj, k % nj
        return o.at[n, pl.ds(pl.multiple_of((1 - c) * half, half), half), pl.ds(pl.multiple_of(j * COLS, COLS), COLS)]

    def c_loc(k):
        s = k % FSLOTS
        return pltpu.make_async_copy(fin.at[s], place(k), ssem.at[KIND["loc"], s])

    def c_out(k):
        s = k % FSLOTS
        return rc("out", s, fin.at[s], place(k), sib)

    def c_out_in(k):
        s = k % FSLOTS
        return rc("out", s, fin.at[s], other_place(k), sib)

    def a0(k):
        s = k % SLOTS
        sb0[s] = acc[k % 2, pl.ds(pl.multiple_of((1 - c) * half, half), half), :].astype(BF16)
        c_core(k).start()

    def a1(k):
        s = k % SLOTS
        c_core(k).wait()

        def total(first, count):
            rows_ = pl.ds(pl.multiple_of(c * half + first * part, part), count * part)
            return acc[k % 2, rows_, :] + rb0[s, pl.ds(pl.multiple_of(first * part, part), count * part), :].astype(F32)

        sby[s] = total(1 - y, 1).astype(BF16)
        c_y(k).start()

        @pl.when(end)
        def _():
            sbq[s] = total(2, 2).astype(BF16)
            c_q(k).start()

        @pl.when(mid)
        def _():
            keep_q[s] = total(2, 2)

        keep_p[s] = total(y, 1)

    def a2t1(k):
        s = k % SLOTS
        c_y(k).wait()

        @pl.when(end)
        def _():
            sbp[s] = (keep_p[s] + ry[s].astype(F32)).astype(BF16)
            c_p(k).start()

        @pl.when(mid)
        def _():
            keep_p[s] += ry[s].astype(F32)

    def a2t2(k):
        s = k % SLOTS

        @pl.when(mid)
        def _():
            c_q(k).wait_recv()
            sbw[s] = (keep_q[s, piece(1 - i), :] + rq[s, piece(1 - i), :].astype(F32)).astype(BF16)
            c_w(k).start()
            keep_w[s] = keep_q[s, piece(i), :] + rq[s, piece(i), :].astype(F32)

        @pl.when(end)
        def _():
            c_q(k).wait_send()

    def a3t1(k):
        s = k % SLOTS

        @pl.when(mid)
        def _():
            c_p(k).wait_recv()
            sbx[s] = (keep_p[s] + rp[s].astype(F32)).astype(BF16)
            c_x(k).start()

        @pl.when(end)
        def _():
            c_p(k).wait_send()

    def a3t2(k):
        s = k % SLOTS

        @pl.when(mid)
        def _():
            c_w(k).wait()
            sbt[s] = (keep_w[s] + rw[s].astype(F32)).astype(BF16)
            c_t(k).start()

    def a4t1(k):
        s = k % SLOTS

        @pl.when(mid)
        def _():
            c_x(k).wait()
            fin[k % FSLOTS, piece(y), :] = (sbx[s].astype(F32) + rx[s].astype(F32)).astype(BF16)
            c_fin("fe1", k, y, outer).start()
            c_fin("fy", k, y, across).start()

    def a4t2(k):
        s = k % SLOTS

        @pl.when(mid)
        def _():
            c_t(k).wait()
            fin[k % FSLOTS, piece(2 + i), :] = (sbt[s].astype(F32) + rt[s].astype(F32)).astype(BF16)
            c_fin("f2m", k, 2 + i, partner).start()
            c_fin("fe2", k, 2 + i, outer).start()

    def a5t1(k):
        @pl.when(end)
        def _():
            c_fin("fe1", k, y, outer).wait_recv()
            c_fin("fy", k, y, across).start()

        @pl.when(mid)
        def _():
            c_fin("fe1", k, y, outer).wait_send()

    def a5t2(k):
        @pl.when(mid)
        def _():
            c_fin("f2m", k, 2 + i, partner).wait_send()
            c_fin("f2m", k, 3 - i, partner).wait_recv()
            c_fin("fe3", k, 3 - i, outer).start()

    def a6(k):
        c_fin("fy", k, y, across).wait_send()
        c_fin("fy", k, 1 - y, across).wait_recv()

        @pl.when(end)
        def _():
            c_fin("fe2", k, 2 + i, outer).wait_recv()
            c_fin("fe3", k, 3 - i, outer).wait_recv()

        c_out(k).start()
        c_loc(k).start()

    def a7(k):
        @pl.when(mid)
        def _():
            c_fin("fe2", k, 2 + i, outer).wait_send()
            c_fin("fe3", k, 3 - i, outer).wait_send()

        c_loc(k).wait()
        c_out(k).wait_send()
        c_out_in(k).wait_recv()

    stages = dict(a1=a1, a2t1=a2t1, a2t2=a2t2, a3t1=a3t1, a3t2=a3t2, a4t1=a4t1, a4t2=a4t2, a5t1=a5t1, a5t2=a5t2, a6=a6, a7=a7)

    for k in range(nk):
        for s in range(per_dot):
            acopy(0, k * per_dot + s).start()
        gcopy(k).start()
    for k in range(nk, GBUFS):
        gcopy(k).start()

    barrier = pltpu.get_barrier_semaphore()

    def greet(dev):
        pl.semaphore_signal(barrier, inc=1, device_id={"dp": dev}, device_id_type=MESH)

    greet(sib)
    greet(across)

    @pl.when(mid)
    def _():
        greet(partner)
        greet(outer)
        pl.semaphore_wait(barrier, 4)

    @pl.when(end)
    def _():
        greet(inner)
        pl.semaphore_wait(barrier, 3)

    def step(t, carry):
        n, j = t // nj, t % nj
        for q in range(nk):
            for name in sorted(LAGS, key=LAGS.get, reverse=True):
                lag = LAGS[name]
                if lag % nk == q:
                    k = t - lag // nk

                    @pl.when((k >= 0) & (k < blocks))
                    def _(name=name, k=k):
                        stages[name](k)

            @pl.when(t < blocks)
            def _():
                s = t * nk + q

                @pl.when(j == 0)
                def _():
                    for r in range(per_dot):
                        acopy(n, q * per_dot + r).wait()

                gcopy(s).wait()
                d = lax.dot_general(
                    abuf[n % 2, pl.ds(q * DEPTH, DEPTH), :], gbuf[s % GBUFS], (((0,), (0,)), ((), ())),
                    preferred_element_type=F32,
                )
                if q == 0:
                    acc[t % 2] = d
                else:
                    acc[t % 2] += d

                @pl.when(s + GBUFS < blocks * nk)
                def _():
                    gcopy(s + GBUFS).start()

        @pl.when((j >= 1) & (j <= ASLABS) & (n + 1 < mats))
        def _():
            acopy(n + 1, j - 1).start()

        @pl.when(t < blocks)
        def _():
            a0(t)

        return carry

    lax.fori_loop(0, blocks + max(LAGS.values()) // nk, step, 0)


def solution(mesh):
    def local(a, g):
        _, mats, tokens, rows = a.shape
        ff = g.shape[3]
        nk = tokens // DEPTH
        half, part = rows // 2, rows // 8

        def sent(count):
            return [pltpu.VMEM((SLOTS, count * part, COLS), BF16)] * 2

        return pl.pallas_call(
            kernel,
            out_shape=jax.ShapeDtypeStruct((mats, rows, ff), BF16),
            in_specs=[pl.BlockSpec(memory_space=pl.ANY)] * 2,
            out_specs=pl.BlockSpec(memory_space=pl.ANY),
            scratch_shapes=[
                pltpu.VMEM((2, tokens, rows), BF16),
                pltpu.VMEM((GBUFS, DEPTH, COLS), BF16),
                pltpu.VMEM((2, rows, COLS), F32),
                *sent(4), *sent(1), *sent(2), *sent(1), *sent(1), *sent(1), *sent(1),
                pltpu.VMEM((FSLOTS, half, COLS), BF16),
                pltpu.VMEM((SLOTS, part, COLS), F32),
                pltpu.VMEM((SLOTS, 2 * part, COLS), F32),
                pltpu.VMEM((SLOTS, part, COLS), F32),
                pltpu.SemaphoreType.DMA((2, ASLABS)),
                pltpu.SemaphoreType.DMA((GBUFS,)),
                pltpu.SemaphoreType.DMA((len(KINDS), FSLOTS)),
                pltpu.SemaphoreType.DMA((len(KINDS), FSLOTS)),
            ],
            compiler_params=pltpu.CompilerParams(
                collective_id=0, has_side_effects=True, vmem_limit_bytes=63 * 2**20
            ),
            cost_estimate=pl.CostEstimate(
                flops=2 * mats * tokens * rows * ff, bytes_accessed=2 * mats * tokens * (rows + ff), transcendentals=0
            ),
        )(a, g)

    group = P(("rep", "dp"))
    return jax.shard_map(local, mesh=mesh, in_specs=(group, group), out_specs=P("rep"), check_vma=False)
```

time: 926 us -> 234 us (0.25)
  blocking collectives: 758 us -> 0 us
  Pallas kernels: 0 us -> 218 us
  matrix products: 167 us -> 0 us
  local copies, waits for them, and re-layouts: 0 us -> 15.6 us
    dot_general x1 -> x0, blocking collectives: 758 us -> none  [step(): jnp.einsum('rsntd,rsntf->rndf', a, g, preferred_element_type=jnp.float32)]
    pallas_call x0 -> x1, Pallas kernels: none -> 218 us  [local(): pl.pallas_call(kernel, out_shape=jax.ShapeDtypeStruct((mats, rows, ff), B...]
    dot_general x1 -> x0, matrix products: 167 us -> none  [step(): jnp.einsum('rsntd,rsntf->rndf', a, g, preferred_element_type=jnp.float32)]
    unnamed x0 -> x1, local copies, waits for them, and re-layouts: none -> 15.6 us
where the time goes in v1:
time: 234 us
  Pallas kernels  218 us (93%)
  local copies, waits for them, and re-layouts  15.6 us (7%)
    pallas_call x1, Pallas kernels, local(): pl.pallas_call(kernel, out_shape=jax.ShapeDtypeStruct((mats, rows, ff), B...  218 us
    unnamed x1, local copies, waits for them, and re-layouts  15.6 us

profile of v1, /device:TPU:0, one launch (start us, length us, event | category | flops | bytes accessed | tf_op | source)
XLA Modules:
  0.0 233.9 jit_solution(4291570545460921847)
XLA Ops:
  0.0 218.3 %shard_map.28 = bf16[4,896,2560]{2,1,0:T(8,128)(2,1)} custom-call(bf16[1,4,8192,896]{3,2,1,0:T(8,128)(2,1)} %a.1, bf16[1,4,8192,2560]{3,2,1,0:T(8,128)(2,1)} %g.1), custom_call_target="tpu_custom_call" | custom-call | flops 150323855360 | bytes 226492416 | tf_op jit(solution)/shard_map/pallas_call | solution.py:342
  218.3 15.6 %copy.4 = bf16[4,896,2560]{2,1,0:T(8,128)(2,1)} copy(bf16[4,896,2560]{2,1,0:T(8,128)(2,1)} %shard_map.28) | data formatting | bytes 36700160

commit v2 on v1

--- a/solution.py
+++ b/solution.py
@@ -15,13 +15,13 @@
 SLOTS = 4
 FSLOTS = 8
 LAGS = dict(a1=3, a2t1=5, a2t2=6, a3t1=7, a3t2=8, a4t1=9, a4t2=10, a5t1=11, a5t2=12, a6=14, a7=16)
-KINDS = ("core", "y", "q", "p", "w", "x", "t", "fe1", "fy", "f2m", "fe2", "fe3", "out", "loc")
+KINDS = ("core", "y", "qf", "qk", "p", "w", "x", "t", "fe1", "fy", "f2m", "fe2", "fe3", "out")
 KIND = {name: i for i, name in enumerate(KINDS)}
 
 
 def kernel(
-    a, g, o, abuf, gbuf, acc, sb0, rb0, sby, ry, sbq, rq, sbp, rp, sbw, rw, sbx, rx, sbt, rt, fin,
-    keep_p, keep_q, keep_w, asem, gsem, ssem, rsem,
+    a, g, o, abuf, gbuf, acc, sb0, rb0, sby, ry, sbq, rq, sbp, rp, sbw, rw, sbx, rx, sbt, rt,
+    keep_p, keep_q, asem, gsem, ssem, rsem,
 ):
     mats, tokens, rows = a.shape[1:]
     ff = g.shape[3]
@@ -74,9 +74,9 @@
         s = k % SLOTS
         return rc("y", s, sby.at[s], ry.at[s], across)
 
-    def c_q(k):
-        s = k % SLOTS
-        return rc("q", s, sbq.at[s], rq.at[s], inner)
+    def c_q(k, which, kind):
+        s = k % SLOTS
+        return rc(kind, s, sbq.at[s, piece(which), :], rq.at[s, piece(which), :], inner)
 
     def c_p(k):
         s = k % SLOTS
@@ -94,29 +94,17 @@
         s = k % SLOTS
         return rc("t", s, sbt.at[s], rt.at[s], across)
 
+    def place(k, first, count):
+        n, j = k // nj, k % nj
+        return n, pl.ds(pl.multiple_of(first * part, part), count * part), pl.ds(pl.multiple_of(j * COLS, COLS), COLS)
+
     def c_fin(kind, k, which, dev):
-        s = k % FSLOTS
-        return rc(kind, s, fin.at[s, piece(which), :], fin.at[s, piece(which), :], dev)
-
-    def place(k):
-        n, j = k // nj, k % nj
-        return o.at[n, pl.ds(pl.multiple_of(c * half, half), half), pl.ds(pl.multiple_of(j * COLS, COLS), COLS)]
-
-    def other_place(k):
-        n, j = k // nj, k % nj
-        return o.at[n, pl.ds(pl.multiple_of((1 - c) * half, half), half), pl.ds(pl.multiple_of(j * COLS, COLS), COLS)]
-
-    def c_loc(k):
-        s = k % FSLOTS
-        return pltpu.make_async_copy(fin.at[s], place(k), ssem.at[KIND["loc"], s])
-
-    def c_out(k):
-        s = k % FSLOTS
-        return rc("out", s, fin.at[s], place(k), sib)
-
-    def c_out_in(k):
-        s = k % FSLOTS
-        return rc("out", s, fin.at[s], other_place(k), sib)
+        at_ = o.at[place(k, 4 * c + which, 1)]
+        return rc(kind, k % FSLOTS, at_, at_, dev)
+
+    def c_out(k, core):
+        at_ = o.at[place(k, 4 * core, 4)]
+        return rc("out", k % FSLOTS, at_, at_, sib)
 
     def a0(k):
         s = k % SLOTS
@@ -137,7 +125,8 @@
         @pl.when(end)
         def _():
             sbq[s] = total(2, 2).astype(BF16)
-            c_q(k).start()
+            c_q(k, 1 - i, "qf").start()
+            c_q(k, i, "qk").start()
 
         @pl.when(mid)
         def _():
@@ -163,14 +152,14 @@
 
         @pl.when(mid)
         def _():
-            c_q(k).wait_recv()
+            c_q(k, 1 - i, "qf").wait_recv()
             sbw[s] = (keep_q[s, piece(1 - i), :] + rq[s, piece(1 - i), :].astype(F32)).astype(BF16)
             c_w(k).start()
-            keep_w[s] = keep_q[s, piece(i), :] + rq[s, piece(i), :].astype(F32)
-
-        @pl.when(end)
-        def _():
-            c_q(k).wait_send()
+
+        @pl.when(end)
+        def _():
+            c_q(k, 1 - i, "qf").wait_send()
+            c_q(k, i, "qk").wait_send()
 
     def a3t1(k):
         s = k % SLOTS
@@ -191,7 +180,8 @@
         @pl.when(mid)
         def _():
             c_w(k).wait()
-            sbt[s] = (keep_w[s] + rw[s].astype(F32)).astype(BF16)
+            c_q(k, i, "qk").wait_recv()
+            sbt[s] = (keep_q[s, piece(i), :] + rq[s, piece(i), :].astype(F32) + rw[s].astype(F32)).astype(BF16)
             c_t(k).start()
 
     def a4t1(k):
@@ -200,7 +190,7 @@
         @pl.when(mid)
         def _():
             c_x(k).wait()
-            fin[k % FSLOTS, piece(y), :] = (sbx[s].astype(F32) + rx[s].astype(F32)).astype(BF16)
+            o[place(k, 4 * c + y, 1)] = (sbx[s].astype(F32) + rx[s].astype(F32)).astype(BF16)
             c_fin("fe1", k, y, outer).start()
             c_fin("fy", k, y, across).start()
 
@@ -210,7 +200,7 @@
         @pl.when(mid)
         def _():
             c_t(k).wait()
-            fin[k % FSLOTS, piece(2 + i), :] = (sbt[s].astype(F32) + rt[s].astype(F32)).astype(BF16)
+            o[place(k, 4 * c + 2 + i, 1)] = (sbt[s].astype(F32) + rt[s].astype(F32)).astype(BF16)
             c_fin("f2m", k, 2 + i, partner).start()
             c_fin("fe2", k, 2 + i, outer).start()
 
@@ -240,8 +230,7 @@
             c_fin("fe2", k, 2 + i, outer).wait_recv()
             c_fin("fe3", k, 3 - i, outer).wait_recv()
 
-        c_out(k).start()
-        c_loc(k).start()
+        c_out(k, c).start()
 
     def a7(k):
         @pl.when(mid)
@@ -249,16 +238,16 @@
             c_fin("fe2", k, 2 + i, outer).wait_send()
             c_fin("fe3", k, 3 - i, outer).wait_send()
 
-        c_loc(k).wait()
-        c_out(k).wait_send()
-        c_out_in(k).wait_recv()
+        c_out(k, c).wait_send()
+        c_out(k, 1 - c).wait_recv()
 
     stages = dict(a1=a1, a2t1=a2t1, a2t2=a2t2, a3t1=a3t1, a3t2=a3t2, a4t1=a4t1, a4t2=a4t2, a5t1=a5t1, a5t2=a5t2, a6=a6, a7=a7)
 
     for k in range(nk):
         for s in range(per_dot):
             acopy(0, k * per_dot + s).start()
-        gcopy(k).start()
+        if k < GBUFS:
+            gcopy(k).start()
     for k in range(nk, GBUFS):
         gcopy(k).start()
 
@@ -333,33 +322,30 @@
     def local(a, g):
         _, mats, tokens, rows = a.shape
         ff = g.shape[3]
-        nk = tokens // DEPTH
-        half, part = rows // 2, rows // 8
+        part = rows // 8
 
         def sent(count):
             return [pltpu.VMEM((SLOTS, count * part, COLS), BF16)] * 2
 
         return pl.pallas_call(
             kernel,
-            out_shape=jax.ShapeDtypeStruct((mats, rows, ff), BF16),
+            out_shape=pltpu.VMEM((mats, rows, ff), BF16),
             in_specs=[pl.BlockSpec(memory_space=pl.ANY)] * 2,
-            out_specs=pl.BlockSpec(memory_space=pl.ANY),
+            out_specs=pl.BlockSpec(memory_space=pltpu.VMEM),
             scratch_shapes=[
                 pltpu.VMEM((2, tokens, rows), BF16),
                 pltpu.VMEM((GBUFS, DEPTH, COLS), BF16),
                 pltpu.VMEM((2, rows, COLS), F32),
                 *sent(4), *sent(1), *sent(2), *sent(1), *sent(1), *sent(1), *sent(1),
-                pltpu.VMEM((FSLOTS, half, COLS), BF16),
                 pltpu.VMEM((SLOTS, part, COLS), F32),
                 pltpu.VMEM((SLOTS, 2 * part, COLS), F32),
-                pltpu.VMEM((SLOTS, part, COLS), F32),
                 pltpu.SemaphoreType.DMA((2, ASLABS)),
                 pltpu.SemaphoreType.DMA((GBUFS,)),
                 pltpu.SemaphoreType.DMA((len(KINDS), FSLOTS)),
                 pltpu.SemaphoreType.DMA((len(KINDS), FSLOTS)),
             ],
             compiler_params=pltpu.CompilerParams(
-                collective_id=0, has_side_effects=True, vmem_limit_bytes=63 * 2**20
+                collective_id=0, has_side_effects=True, vmem_limit_bytes=45 * 2**20
             ),
             cost_estimate=pl.CostEstimate(
                 flops=2 * mats * tokens * rows * ff, bytes_accessed=2 * mats * tokens * (rows + ff), transcendentals=0

time: 234 us -> 226 us (0.966)
  local copies, waits for them, and re-layouts: 15.6 us -> 6.68 us
    unnamed x1, local copies, waits for them, and re-layouts: 15.6 us -> 6.68 us
where the time goes in v2:
time: 226 us
  Pallas kernels  219 us (97%)
  local copies, waits for them, and re-layouts  6.68 us (3%)
    pallas_call x1, Pallas kernels, local(): pl.pallas_call(kernel, out_shape=pltpu.VMEM((mats, rows, ff), BF16), in_s...  219 us
    unnamed x1, local copies, waits for them, and re-layouts  6.68 us

profile of v2, /device:TPU:0, one launch (start us, length us, event | category | flops | bytes accessed | tf_op | source)
XLA Modules:
  0.0 226.1 jit_solution(1272054394156098628)
XLA Ops:
  0.0 219.4 %shard_map.28 = bf16[4,896,2560]{2,1,0:T(8,128)(2,1)S(1)} custom-call(bf16[1,4,8192,896]{3,2,1,0:T(8,128)(2,1)} %a.1, bf16[1,4,8192,2560]{3,2,1,0:T(8,128)(2,1)} %g.1), custom_call_target="tpu_custom_call" | custom-call | flops 150323855360 | bytes 226492416 | tf_op jit(solution)/shard_map/pallas_call | solution.py:330
  219.4 6.7 %copy.4 = bf16[4,896,2560]{2,1,0:T(8,128)(2,1)} copy(bf16[4,896,2560]{2,1,0:T(8,128)(2,1)S(1)} %shard_map.28) | data formatting | bytes 36700160
